TPU v7x, 32 devices: a whole 2x2x4 slice. The times are simulated.
32 devices in a mesh: samp: 4 (over x, core), feat: 8 (over z, y).
Axes of the slice: x: 2, y: 2, z: 4, core: 2. Of those that a mesh axis runs over, the one named last changes fastest.
Arguments:
- design: float32 [4096, 65536], P('samp', 'feat'), may hold values from -0.09375 to 0.09375
- coefficients: float32 [192, 65536], P(None, 'feat'), may hold values from -3 to 3
- response: float32 [192, 4096], P(None, 'samp'), may hold values from -6 to 6
- active_set: int32 [192, 65536], P(None, 'feat'), may hold values 0 or 1
- lambda_path: float32 [192, 16], P('samp'), may hold values from 0.5 to 4
- lambda_index: int32 [192], P('samp'), may hold values from 1 to 15
Outputs:
- margins: float32 [192, 65536], P('samp', 'feat')
- peak_gradient: float32 [192], P('samp')
- violation: float32 [192], P('samp')
- screen_mass: float32 [192], P('samp')
Inputs may be any that keep to these rules, and one draw needn't show every extreme that they name: `active_set`: 1 marks a feature in the response's active set, 0 one outside it. `lambda_index`: the current point on the response's path; the previous point is the one just below it.
All inputs are finite; a program needn't handle non-finite values. No bound on the sum of `active_set` on one device may be relied on, other than what follows from the above.
Results may differ from a plain program's by a relative error of at most 0.000073.
Values sent between devices are 32-bit elements; how exact they have to be, the bound alone decides.
A program may use at most 128 MiB of HBM per device.

v0:
```python
import jax
import jax.numpy as jnp
from jax import lax
from jax.sharding import PartitionSpec as P

NF = 65536


def body(design, coefficients, response, active_set, lambda_path, lambda_index):
    masked = coefficients * active_set.astype(jnp.float32)
    partial_value = lax.dot_general(
        masked,
        design,
        (((1,), (1,)), ((), ())),
        precision=lax.Precision.HIGHEST,
        preferred_element_type=jnp.float32,
    )
    fitted = lax.psum(partial_value, "feat")
    residual = response - fitted
    share_rows = lambda_path.shape[0]
    own_first = lax.axis_index("samp") * share_rows
    gradient = lax.psum_scatter(
        jnp.dot(
            residual, design, precision=lax.Precision.HIGHEST, preferred_element_type=jnp.float32
        ),
        "samp",
        scatter_dimension=0,
        tiled=True,
    )
    own_active = lax.dynamic_slice_in_dim(active_set, own_first, share_rows, 0)
    positions = jnp.arange(lambda_path.shape[1], dtype=jnp.int32)
    picker_now = (positions[None, :] == lambda_index[:, None]).astype(jnp.float32)
    picker_before = (positions[None, :] == lambda_index[:, None] - 1).astype(jnp.float32)
    lambda_new = jnp.sum(lambda_path * picker_now, axis=1)
    lambda_old = jnp.sum(lambda_path * picker_before, axis=1)
    threshold = 2.0 * lambda_new - lambda_old
    magnitude = jnp.abs(gradient)
    margins = magnitude - threshold[:, None]
    local_peak = jnp.max(magnitude, axis=1)
    inactive = 1.0 - own_active.astype(jnp.float32)
    local_violation = (
        jnp.sum(inactive * jnp.maximum(magnitude - lambda_new[:, None], 0.0), axis=1) / NF
    )
    local_mass = jnp.sum(jnp.maximum(margins, 0.0), axis=1) / NF
    peak_gradient = lax.pmax(local_peak, "feat")
    violation, screen_mass = lax.psum((local_violation, local_mass), "feat")
    return (margins, peak_gradient, violation, screen_mass)


def solution(mesh):
    return jax.shard_map(
        body,
        mesh=mesh,
        in_specs=(
            P("samp", "feat"),
            P(None, "feat"),
            P(None, "samp"),
            P(None, "feat"),
            P("samp", None),
            P("samp"),
        ),
        out_specs=(P("samp", "feat"), P("samp"), P("samp"), P("samp")),
        check_vma=False,
    )
```

profile of v0, /device:TPU:0, one launch (start us, length us, event | category | flops | bytes accessed | tf_op | source)
XLA Modules:
  0.0 260.9 jit_solution(6805318242318605775)
XLA Ops:
  7.2 0.0 copy-start
  7.2 0.0 all-reduce.3.cloned.1.call-start
  7.2 39.6 %fusion = f32[192,1024]{1,0:T(8,128)} fusion(f32[1024,8192]{1,0:T(8,128)} %param.6, f32[192,8192]{1,0:T(8,128)} %param.7, s32[192,8192]{1,0:T(8,128)} %param.9), kind=kOutput, calls=%fused_computation | convolution fusion | flops 19330498560 | bytes 46923776 | tf_op jit(solution)/shard_map/dot_general | solution.py:11
  46.8 0.0 all-reduce.3.cloned.1.call-update
  46.8 0.2 reduce-scatter.2.cloned.1.call-start
  47.0 77.7 %all-reduce.3.cloned.1.call-done = f32[192,1024]{1,0:T(8,128)} async-done(((f32[192,1024]{1,0:T(8,128)}), f32[192,1024]{1,0:T(8,128)}) %all-reduce.3.cloned.1.call-update) | async-done | bytes 786448 | tf_op jit(solution)/shard_map/psum | solution.py:18
  124.8 0.0 copy-done
  124.8 27.9 %fusion.3 = f32[192,8192]{1,0:T(8,128)} fusion(f32[1024,8192]{1,0:T(8,128)} %param.6, f32[192,1024]{1,0:T(8,128)S(1)} %copy-done, f32[192,1024]{1,0:T(8,128)} %all-reduce.3.cloned.1.call-done), kind=kOutput, calls=%fused_computation.7 | convolution fusion | flops 19327549440 | bytes 41418752 | tf_op jit(solution)/shard_map/dot_general | solution.py:23
  152.7 0.0 copy-start.2
  152.7 0.0 copy-start.1
  152.7 0.0 reduce-scatter.2.cloned.1.call-update
  152.7 0.6 copy-done.2
  153.3 0.1 copy-done.1
  153.4 57.4 %reduce-scatter.2.cloned.1.call-done = f32[48,8192]{1,0:T(8,128)} async-done(((f32[192,8192]{1,0:T(8,128)}), f32[48,8192]{1,0:T(8,128)}) %reduce-scatter.2.cloned.1.call-update) | async-done | bytes 1572880 | tf_op jit(solution)/shard_map/reduce_scatter | solution.py:22
  210.9 3.7 %multiply_reduce_fusion = (f32[48]{0:T(128)S(1)}, f32[48]{0:T(128)S(1)}, f32[48]{0:T(128)S(1)}, f32[48,8192]{1,0:T(8,128)}) fusion(s32[192,8192]{1,0:T(8,128)} %param.9, s32[]{:T(128)S(6)} %select_n.3, f32[48,8192]{1,0:T(8,128)} %reduce-scatter.2.cloned.1.call-done, f32[48]{0:T(128)S(1)} %get-tuple-element.6, f32[48]{0:T(128)S(1)} %multiply_subtract_fusion), kind=kLoop, calls=%fused_computation.4 | loop fusion | flops 4325232 | bytes 4719556 | tf_op jit(solution)/shard_map/reduce_sum | solution.py:42
  214.6 21.9 %pmax.7 = f32[48]{0:T(128)} all-reduce(f32[48]{0:T(128)S(1)} %get-tuple-element.5), channel_id=1, replica_groups=mesh['samp'=4,'feat'=8] {'feat'}, use_global_device_ids=true, to_apply=%region_5.0 | all-reduce | flops 48 | bytes 384 | tf_op jit(solution)/shard_map/pmax | solution.py:45
  236.5 17.6 %all-reduce = (f32[48]{0:T(128)}, f32[48]{0:T(128)}) all-reduce(f32[48]{0:T(128)S(1)} %get-tuple-element.15, f32[48]{0:T(128)S(1)} %get-tuple-element.14), channel_id=1, replica_groups=mesh['samp'=4,'feat'=8] {'feat'}, use_global_device_ids=true, to_apply=%region_7.0 | all-reduce | flops 96 | bytes 768 | tf_op jit(solution)/shard_map/psum | solution.py:46
  (4 shorter events, 0.0 us)
Async XLA Ops:
  7.2 117.6 %copy-start = (f32[192,1024]{1,0:T(8,128)S(1)}, f32[192,1024]{1,0:T(8,128)}, u32[]{:S(2)}) copy-start(f32[192,1024]{1,0:T(8,128)} %param.8) | copy-start | bytes 2359300
  7.2 117.6 %all-reduce.3.cloned.1.call-start = ((), (), s32[]{:S(2)}) async-start(), calls=%async_computation.1 | async-start | bytes 1572864 | tf_op jit(solution)/shard_map/psum | solution.py:18
  46.8 164.1 %reduce-scatter.2.cloned.1.call-start = ((), (), s32[]{:S(2)}) async-start(), calls=%async_computation.2 | async-start | bytes 7864320 | tf_op jit(solution)/shard_map/reduce_scatter | solution.py:22
  152.7 0.7 copy-start.2
  152.7 0.7 copy-start.1
Sparse Core Ops, SparseCore 0:
  46.9 77.7 all-reduce.2
  152.8 57.9 reduce-scatter.1
where the time goes:
time: 261 us
  waiting for transfers between devices  135 us (52%)
  matrix products  67.5 us (26%)
  blocking collectives  39.5 us (15%)
  between operations  14.1 us (5%)
  other arithmetic  3.78 us (1%)
    psum x1, waiting for transfers between devices, body(): fitted = lax.psum(partial_value, 'feat')  77.7 us
    reduce_scatter x1, waiting for transfers between devices, body(): lax.psum_scatter(jnp.dot(residual, design, precision=lax.Precision.HIGHES...  57.4 us
    dot_general x1, matrix products, body(): lax.dot_general(masked, design, (((1,), (1,)), ((), ())), precision=lax.P...  39.6 us
    dot_general x1, matrix products, body(): jnp.dot(residual, design, precision=lax.Precision.HIGHEST, preferred_elem...  27.9 us
    pmax x1, blocking collectives, body(): peak_gradient = lax.pmax(local_peak, 'feat')  21.9 us
    psum x1, blocking collectives, body(): violation, screen_mass = lax.psum((local_violation, local_mass), 'feat')  17.6 us
  transfers between devices with their start and end apart: 2, of which 2 were waited for; matrix products, arithmetic and copies ran while one was open for 0% of the time, Pallas kernels for 0%

commit v1 on v0

--- a/solution.py
+++ b/solution.py
@@ -15,7 +15,7 @@
         precision=lax.Precision.HIGHEST,
         preferred_element_type=jnp.float32,
     )
-    fitted = lax.psum(partial_value, "feat")
+    fitted = jnp.sum(lax.all_gather(partial_value, "feat"), axis=0)
     residual = response - fitted
     share_rows = lambda_path.shape[0]
     own_first = lax.axis_index("samp") * share_rows

time: 261 us -> 287 us (1.100)
  waiting for transfers between devices: 135 us -> 158 us
  other arithmetic: 3.78 us -> 7.3 us
    all_gather x0 -> x1, waiting for transfers between devices: none -> 101 us  [body(): fitted = jnp.sum(lax.all_gather(partial_value, 'feat'), axis=0)]
    psum x1 -> x0, waiting for transfers between devices: 77.7 us -> none  [body(): fitted = lax.psum(partial_value, 'feat')]
    reduce_sum x0 -> x1, other arithmetic: none -> 3.52 us  [body(): fitted = jnp.sum(lax.all_gather(partial_value, 'feat'), axis=0)]
where the time goes in v1:
time: 287 us
  waiting for transfers between devices  158 us (55%)
  matrix products  67.3 us (23%)
  blocking collectives  39.5 us (14%)
  between operations  14.1 us (5%)
  other arithmetic  7.3 us (3%)
    all_gather x1, waiting for transfers between devices, body(): fitted = jnp.sum(lax.all_gather(partial_value, 'feat'), axis=0)  101 us
    reduce_scatter x1, waiting for transfers between devices, body(): lax.psum_scatter(jnp.dot(residual, design, precision=lax.Precision.HIGHES...  56.5 us
    dot_general x1, matrix products, body(): lax.dot_general(masked, design, (((1,), (1,)), ((), ())), precision=lax.P...  39.5 us
    dot_general x1, matrix products, body(): jnp.dot(residual, design, precision=lax.Precision.HIGHEST, preferred_elem...  27.8 us
    pmax x1, blocking collectives, body(): peak_gradient = lax.pmax(local_peak, 'feat')  21.9 us
    psum x1, blocking collectives, body(): violation, screen_mass = lax.psum((local_violation, local_mass), 'feat')  17.6 us
  transfers between devices with their start and end apart: 2, of which 2 were waited for; matrix products, arithmetic and copies ran while one was open for 0% of the time, Pallas kernels for 0%

profile of v1, /device:TPU:0, one launch (start us, length us, event | category | flops | bytes accessed | tf_op | source)
XLA Modules:
  0.0 286.9 jit_solution(16531339173735224070)
XLA Ops:
  7.2 0.0 all-gather.3.cloned.1.call-start
  7.2 39.5 %fusion = f32[192,1024]{1,0:T(8,128)} fusion(f32[1024,8192]{1,0:T(8,128)} %param.6, f32[192,8192]{1,0:T(8,128)} %param.7, s32[192,8192]{1,0:T(8,128)} %param.9), kind=kOutput, calls=%fused_computation | convolution fusion | flops 19330498560 | bytes 46923776 | tf_op jit(solution)/shard_map/dot_general | solution.py:11
  46.7 0.0 copy-start
  46.7 0.0 all-gather.3.cloned.1.call-update
  46.7 0.2 reduce-scatter.2.cloned.1.call-start
  47.0 101.3 %all-gather.3.cloned.1.call-done = f32[1536,1024]{1,0:T(8,128)} async-done(((f32[192,1024]{1,0:T(8,128)}), f32[1536,1024]{1,0:T(8,128)}) %all-gather.3.cloned.1.call-update) | async-done | bytes 6291472 | tf_op jit(solution)/shard_map/all_gather | solution.py:18
  148.3 3.5 %reduce_sum.45 = f32[192,1024]{1,0:T(8,128)S(1)} reduce(f32[8,192,1024]{2,1,0:T(8,128)} %bitcast.3, f32[]{:T(128)} %constant.10.clone.1), dimensions={0}, to_apply=%region_0.0 | reduce | flops 1376256 | bytes 7077892 | tf_op jit(solution)/shard_map/reduce_sum | solution.py:18
  151.8 0.0 copy-done
  151.8 27.8 %fusion.3 = f32[192,8192]{1,0:T(8,128)} fusion(f32[1024,8192]{1,0:T(8,128)} %param.6, f32[192,1024]{1,0:T(8,128)S(1)} %copy-done, f32[192,1024]{1,0:T(8,128)S(1)} %reduce_sum.45), kind=kOutput, calls=%fused_computation.7 | convolution fusion | flops 19327549440 | bytes 41418752 | tf_op jit(solution)/shard_map/dot_general | solution.py:23
  179.6 0.0 copy-start.2
  179.6 0.0 copy-start.1
  179.6 0.0 reduce-scatter.2.cloned.1.call-update
  179.6 0.6 copy-done.2
  180.3 0.1 copy-done.1
  180.4 56.5 %reduce-scatter.2.cloned.1.call-done = f32[48,8192]{1,0:T(8,128)} async-done(((f32[192,8192]{1,0:T(8,128)}), f32[48,8192]{1,0:T(8,128)}) %reduce-scatter.2.cloned.1.call-update) | async-done | bytes 1572880 | tf_op jit(solution)/shard_map/reduce_scatter | solution.py:22
  236.8 3.7 %multiply_reduce_fusion = (f32[48]{0:T(128)S(1)}, f32[48]{0:T(128)S(1)}, f32[48]{0:T(128)S(1)}, f32[48,8192]{1,0:T(8,128)}) fusion(s32[192,8192]{1,0:T(8,128)} %param.9, s32[]{:T(128)S(6)} %select_n.3, f32[48,8192]{1,0:T(8,128)} %reduce-scatter.2.cloned.1.call-done, f32[48]{0:T(128)S(1)} %get-tuple-element.6, f32[48]{0:T(128)S(1)} %multiply_subtract_fusion), kind=kLoop, calls=%fused_computation.4 | loop fusion | flops 4325232 | bytes 4719556 | tf_op jit(solution)/shard_map/reduce_sum | solution.py:42
  240.6 21.9 %pmax.7 = f32[48]{0:T(128)} all-reduce(f32[48]{0:T(128)S(1)} %get-tuple-element.5), channel_id=1, replica_groups=mesh['samp'=4,'feat'=8] {'feat'}, use_global_device_ids=true, to_apply=%region_5.0 | all-reduce | flops 48 | bytes 384 | tf_op jit(solution)/shard_map/pmax | solution.py:45
  262.5 17.6 %all-reduce = (f32[48]{0:T(128)}, f32[48]{0:T(128)}) all-reduce(f32[48]{0:T(128)S(1)} %get-tuple-element.15, f32[48]{0:T(128)S(1)} %get-tuple-element.14), channel_id=1, replica_groups=mesh['samp'=4,'feat'=8] {'feat'}, use_global_device_ids=true, to_apply=%region_7.0 | all-reduce | flops 96 | bytes 768 | tf_op jit(solution)/shard_map/psum | solution.py:46
  (4 shorter events, 0.0 us)
Async XLA Ops:
  7.2 141.2 %all-gather.3.cloned.1.call-start = ((), (), s32[]{:S(2)}) async-start(), calls=%async_computation.2 | async-start | bytes 7077888 | tf_op jit(solution)/shard_map/all_gather | solution.py:18
  46.7 105.1 %copy-start = (f32[192,1024]{1,0:T(8,128)S(1)}, f32[192,1024]{1,0:T(8,128)}, u32[]{:S(2)}) copy-start(f32[192,1024]{1,0:T(8,128)} %param.8) | copy-start | bytes 2359300
  46.7 190.1 %reduce-scatter.2.cloned.1.call-start = ((), (), s32[]{:S(2)}) async-start(), calls=%async_computation.1 | async-start | bytes 7864320 | tf_op jit(solution)/shard_map/reduce_scatter | solution.py:22
  179.6 0.7 copy-start.2
  179.6 0.7 copy-start.1
Sparse Core Ops, SparseCore 0:
  46.9 101.4 all-gather.2
  179.8 57.0 reduce-scatter.1
